TPU v7x, 32 devices: a whole 2x2x4 slice. The times are simulated.
32 devices in a mesh: ty: 4 (over y, x), tx: 8 (over z, core).
Axes of the slice: x: 2, y: 2, z: 4, core: 2. Of those that a mesh axis runs over, the one named last changes fastest.
Arguments:
- object_slices: float32 [2, 2, 1024, 2048], P(None, None, 'ty', 'tx'), may hold values from -5 to 5
- probe: float32 [2, 256, 256], replicated, may hold values from -5 to 5
- position_count: int32 [4, 8], P('ty', 'tx'), may hold values from 1 to 5, as said below
- offsets: int32 [4, 8, 5, 2], P('ty', 'tx'), may hold values from 0 to 128
- intensities: float32 [4, 8, 5, 256, 256], P('ty', 'tx'), may hold values from 0 to 2
Outputs:
- object_new: float32 [2, 2, 1024, 2048], P(None, None, 'ty', 'tx')
- probe_new: float32 [2, 256, 256], replicated
Inputs may be any that keep to these rules, and one draw needn't show every extreme that they name: `position_count`: each tile has 1 to 5 positions; some tile has exactly 5.
All inputs are finite; a program needn't handle non-finite values.
Results may differ from a plain program's by a relative error of at most 0.0003.
Values sent between devices are 32-bit elements; how exact they have to be, the bound alone decides.
No kernel may reach another device: no remote copies, remote signals or barrier semaphores. Data moves between devices by JAX's collectives and lax.ppermute only.
A program may use at most 128 MiB of HBM per device.

v0:
```python
import math
import jax
import jax.numpy as jnp
from jax import lax
from jax.sharding import PartitionSpec as P

PROBE = 256
CORE = 256
MARGIN = 64
ITERS = 2
chirp_rate = 0.5
object_rate = 0.5
probe_rate = 2.0


def extended_2(block, sides, width):
    for axis, dim in sides:
        count = lax.axis_size(axis)
        forward = [(i, i + 1) for i in range(count - 1)]
        forward.append((count - 1, 0))
        backward = [(target, source) for source, target in forward]
        low = lax.ppermute(
            lax.slice_in_dim(block, block.shape[dim] - width, None, axis=dim), axis, forward
        )
        high = lax.ppermute(lax.slice_in_dim(block, 0, width, axis=dim), axis, backward)
        block = jnp.concatenate([low, block, high], axis=dim)
    return block


def matmul(left, right):
    return jnp.dot(left, right, precision=lax.Precision.HIGHEST, preferred_element_type=jnp.float32)


def complex_product(left_real, left_imag, right_real, right_imag):
    out_real = matmul(left_real, right_real) - matmul(left_imag, right_imag)
    out_imag = matmul(left_real, right_imag) + matmul(left_imag, right_real)
    return (out_real, out_imag)


def dft_tables(size):
    index = lax.iota(jnp.int32, size)
    product = index[:, None] * index[None, :] % size
    angles = product.astype(jnp.float32) * (2.0 * math.pi / size)
    factor = 1.0 / math.sqrt(size)
    four_real = jnp.cos(angles) * factor
    four_imag = -jnp.sin(angles) * factor
    centred = ((index + size // 2) % size - size // 2).astype(jnp.float32)
    phases = centred * centred * (chirp_rate * math.pi / size)
    kernel_real = jnp.cos(phases)
    kernel_imag = -jnp.sin(phases)
    scaled_real = four_real * kernel_real[None, :] + four_imag * kernel_imag[None, :]
    scaled_imag = four_real * kernel_imag[None, :] - four_imag * kernel_real[None, :]
    prop_real, prop_imag = complex_product(scaled_real, scaled_imag, four_real, four_imag)
    return (four_real, four_imag, prop_real, prop_imag)


def forward_pair(mat_real, mat_imag, field_real, field_imag):
    mid_real, mid_imag = complex_product(mat_real, mat_imag, field_real, field_imag)
    return complex_product(mid_real, mid_imag, mat_real.T, mat_imag.T)


def adjoint_pair(mat_real, mat_imag, field_real, field_imag):
    mid_real, mid_imag = complex_product(mat_real.T, -mat_imag.T, field_real, field_imag)
    return complex_product(mid_real, mid_imag, mat_real, -mat_imag)


def position_grad(probe_now, window, measured, tables):
    four_real, four_imag, prop_real, prop_imag = tables
    probe_real, probe_imag = (probe_now[0], probe_now[1])
    one_real, one_imag, two_real, two_imag = (window[0], window[1], window[2], window[3])
    wave_real = probe_real * one_real - probe_imag * one_imag
    wave_imag = probe_real * one_imag + probe_imag * one_real
    moved_real, moved_imag = forward_pair(prop_real, prop_imag, wave_real, wave_imag)
    exit_real = moved_real * two_real - moved_imag * two_imag
    exit_imag = moved_real * two_imag + moved_imag * two_real
    far_real, far_imag = forward_pair(four_real, four_imag, exit_real, exit_imag)
    misfit = far_real * far_real + far_imag * far_imag - measured
    back_real, back_imag = adjoint_pair(four_real, four_imag, misfit * far_real, misfit * far_imag)
    grad_two_real = moved_real * back_real + moved_imag * back_imag
    grad_two_imag = moved_real * back_imag - moved_imag * back_real
    gmove_real = two_real * back_real + two_imag * back_imag
    gmove_imag = two_real * back_imag - two_imag * back_real
    gwave_real, gwave_imag = adjoint_pair(prop_real, prop_imag, gmove_real, gmove_imag)
    grad_one_real = probe_real * gwave_real + probe_imag * gwave_imag
    grad_one_imag = probe_real * gwave_imag - probe_imag * gwave_real
    gprobe_real = one_real * gwave_real + one_imag * gwave_imag
    gprobe_imag = one_real * gwave_imag - one_imag * gwave_real
    object_part = jnp.stack([grad_one_real, grad_one_imag, grad_two_real, grad_two_imag])
    return (object_part, jnp.stack([gprobe_real, gprobe_imag]))


def fold_axis(padded, width, dim):
    extent = padded.shape[dim] - 2 * width
    middle = lax.slice_in_dim(padded, width, width + extent, axis=dim)
    before = lax.slice_in_dim(padded, 0, width, axis=dim)
    after = lax.slice_in_dim(padded, width + extent, extent + 2 * width, axis=dim)
    spec_before = [(0, 0)] * padded.ndim
    spec_before[dim] = (2 * MARGIN - width, extent - 2 * MARGIN)
    spec_after = [(0, 0)] * padded.ndim
    spec_after[dim] = (CORE, extent - CORE - width)
    return middle + jnp.pad(before, spec_before) + jnp.pad(after, spec_after)


def fold_sums(padded, width):
    return fold_axis(fold_axis(padded, width, 1), width, 2)


def body(object_slices, probe, position_count, offsets, intensities):
    tables = dft_tables(PROBE)
    extent = CORE + 2 * MARGIN
    zero = jnp.int32(0)
    count = position_count[0, 0]
    core = object_slices.reshape(4, CORE, CORE)
    extended = extended_2(core, (("ty", 1), ("tx", 2)), MARGIN)
    probe_now = probe
    devices = lax.axis_size("ty") * lax.axis_size("tx")
    for step in range(ITERS):

        def visit(slot, carry):
            local, local_probe = carry
            top = offsets[0, 0, slot, 0]
            left = offsets[0, 0, slot, 1]
            window = lax.dynamic_slice(extended, (zero, top, left), (4, PROBE, PROBE))
            object_part, probe_part = position_grad(
                probe_now, window, intensities[0, 0, slot], tables
            )
            current = lax.dynamic_slice(local, (zero, top, left), (4, PROBE, PROBE))
            local = lax.dynamic_update_slice(local, current + object_part, (zero, top, left))
            return (local, local_probe + probe_part)

        start = (
            jnp.zeros((4, extent, extent), jnp.float32),
            jnp.zeros((2, PROBE, PROBE), jnp.float32),
        )
        grads, probe_grad = lax.fori_loop(zero, count, visit, start)
        peak = jnp.max(probe_now[0] * probe_now[0] + probe_now[1] * probe_now[1]) + 1e-06
        padded = extended_2(grads, (("ty", 1), ("tx", 2)), MARGIN)
        total = fold_sums(padded, MARGIN)[:, MARGIN : MARGIN + CORE, MARGIN : MARGIN + CORE]
        core = core - object_rate / peak * total
        if step + 1 < ITERS:
            extended = extended_2(core, (("ty", 1), ("tx", 2)), MARGIN)
        summed = lax.psum(probe_grad, ("ty", "tx"))
        probe_now = probe_now - probe_rate / devices * summed
    return (core.reshape(2, 2, CORE, CORE), probe_now)


def solution(mesh):
    placed = (
        P(None, None, "ty", "tx"),
        P(),
        P("ty", "tx"),
        P("ty", "tx", None, None),
        P("ty", "tx", None, None, None),
    )
    return jax.shard_map(
        body,
        mesh=mesh,
        in_specs=placed,
        out_specs=(P(None, None, "ty", "tx"), P()),
        check_vma=False,
    )
```

profile of v0, /device:TPU:0, one launch (start us, length us, event | category | flops | bytes accessed | tf_op | source)
XLA Modules:
  0.0 1035.9 jit_solution(13837448059332774943)
XLA Ops:
  10.0 3.0 collective-permute-start
  17.1 9.8 collective-permute-done
  26.9 10.6 %collective-permute-done.1 = f32[4,64,256]{1,2,0:T(8,128)S(1)} collective-permute-done((f32[4,64,256]{1,2,0:T(8,128)}, f32[4,64,256]{1,2,0:T(8,128)S(1)}, u32[]{:S(2)}, u32[]{:S(2)}) %collective-permute-start.1) | collective-permute-done | bytes 262176 | tf_op jit(solution)/shard_map/ppermute | solution.py:25
  38.0 3.5 collective-permute-start.3
  44.5 4.6 collective-permute-done.2
  49.1 3.1 pad_maximum_fusion.2
  54.6 203.5 %while.32 = (s32[]{:T(128)}, f32[4,384,384]{2,1,0:T(8,128)}, f32[2,256,256]{2,1,0:T(8,128)}, s32[]{:T(128)}, s32[1,1,5,2]{2,3,1,0:T(2,128)S(1)}, /*index=5*/f32[...) while((s32[]{:T(128)}, f32[4,384,384]{2,1,0:T(8,128)}, ...), condition=%wide.region_2.3_spmd.clone.clone, body=%wide.region_1.2_spmd.clone.clone.sunk | while | flops 6464077824 | bytes 48234916 | solution.py:135
  83.4 2.5 fusion.635
  103.6 2.4 fusion.646
  125.1 11.5 %dynamic_update_slice.16 = f32[4,384,384]{2,1,0:T(8,128)} dynamic-update-slice(f32[4,384,384]{2,1,0:T(8,128)} %get-tuple-element.1014, f32[4,256,256]{2,1,0:T(8,128)S(1)} %maximum_add_fusion.8, s32[]{:T(128)} %constant.70.clone.1..sunk, s32[]{:T(128)S(6)} %select_n.366, s32[]{:T(128)S(6)} %select_n.367) | dynamic-update-slice | bytes 2097156 | tf_op jit(solution)/shard_map/while/body/dynamic_update_slice | solution.py:128
  141.4 2.5 fusion.635
  161.7 2.4 fusion.646
  183.1 11.3 %dynamic_update_slice.16 = f32[4,384,384]{2,1,0:T(8,128)} dynamic-update-slice(f32[4,384,384]{2,1,0:T(8,128)} %get-tuple-element.1014, f32[4,256,256]{2,1,0:T(8,128)S(1)} %maximum_add_fusion.8, s32[]{:T(128)} %constant.70.clone.1..sunk, s32[]{:T(128)S(6)} %select_n.366, s32[]{:T(128)S(6)} %select_n.367) | dynamic-update-slice | bytes 2097156 | tf_op jit(solution)/shard_map/while/body/dynamic_update_slice | solution.py:128
  199.2 2.5 fusion.635
  219.5 2.4 fusion.646
  240.9 11.5 %dynamic_update_slice.16 = f32[4,384,384]{2,1,0:T(8,128)} dynamic-update-slice(f32[4,384,384]{2,1,0:T(8,128)} %get-tuple-element.1014, f32[4,256,256]{2,1,0:T(8,128)S(1)} %maximum_add_fusion.8, s32[]{:T(128)} %constant.70.clone.1..sunk, s32[]{:T(128)S(6)} %select_n.366, s32[]{:T(128)S(6)} %select_n.367) | dynamic-update-slice | bytes 2097156 | tf_op jit(solution)/shard_map/while/body/dynamic_update_slice | solution.py:128
  259.3 117.1 %collective-permute-start.5 = (f32[4,64,384]{2,1,0:T(8,128)S(1)}, f32[4,64,384]{2,1,0:T(8,128)S(1)}, u32[]{:S(2)}, u32[]{:S(2)}) collective-permute-start(f32[4,64,384]{2,1,0:T(8,128)S(1)} %get-tuple-element.749), channel_id=1, source_target_pairs={{8,0},{16,8},{24,16},{0,24},{9,1},{17,9},{25,17},{1,25},{10,2},{18... | collective-permute-start | bytes 1179656 | tf_op jit(solution)/shard_map/ppermute | solution.py:25
  376.4 3.1 copy.25
  379.5 4.3 collective-permute-done.4
  386.2 2.5 pad_maximum_fusion.9
  388.7 4.3 collective-permute-start.6
  394.3 7.8 collective-permute-done.6
  402.2 2.7 collective-permute-done.7
  404.9 3.0 pad_maximum_fusion
  408.0 2.8 fusion.242
  413.8 8.9 collective-permute-start.8
  422.7 13.3 %collective-permute-done.8 = f32[4,64,256]{1,2,0:T(8,128)S(1)} collective-permute-done((f32[4,64,256]{1,2,0:T(8,128)}, f32[4,64,256]{1,2,0:T(8,128)S(1)}, u32[]{:S(2)}, u32[]{:S(2)}) %collective-permute-start.8) | collective-permute-done | bytes 262176 | tf_op jit(solution)/shard_map/ppermute | solution.py:22
  436.0 11.2 %collective-permute-done.9 = f32[4,64,256]{1,2,0:T(8,128)} collective-permute-done((f32[4,64,256]{1,2,0:T(8,128)}, f32[4,64,256]{1,2,0:T(8,128)}, u32[]{:S(2)}, u32[]{:S(2)}) %collective-permute-start.9) | collective-permute-done | bytes 262176 | tf_op jit(solution)/shard_map/ppermute | solution.py:25
  449.4 3.5 collective-permute-start.11
  452.9 100.7 %all-reduce.11.cloned.1.call-done = f32[2,256,256]{2,1,0:T(8,128)} async-done(((f32[2,256,256]{2,1,0:T(8,128)}), f32[2,256,256]{2,1,0:T(8,128)}) %all-reduce.11.cloned.1.call-update) | async-done | bytes 524304 | tf_op jit(solution)/shard_map/psum | solution.py:142
  554.7 3.3 pad_maximum_fusion.3
  560.5 204.1 %while.33 = (s32[]{:T(128)}, f32[4,384,384]{2,1,0:T(8,128)}, f32[2,256,256]{2,1,0:T(8,128)}, s32[]{:T(128)}, s32[1,1,5,2]{2,3,1,0:T(2,128)S(1)}, /*index=5*/f32[...) while((s32[]{:T(128)}, f32[4,384,384]{2,1,0:T(8,128)}, ...), condition=%wide.region_6.7_spmd.clone.clone, body=%wide.region_5.6_spmd.clone.clone.sunk | while | flops 6464077824 | bytes 48234916 | solution.py:135
  589.1 2.5 fusion.709
  609.4 2.4 fusion.720
  631.4 11.5 %dynamic_update_slice.17 = f32[4,384,384]{2,1,0:T(8,128)} dynamic-update-slice(f32[4,384,384]{2,1,0:T(8,128)} %get-tuple-element.1071, f32[4,256,256]{2,1,0:T(8,128)S(1)} %maximum_add_fusion.10, s32[]{:T(128)} %constant.70.clone.1..sunk.1, s32[]{:T(128)S(6)} %select_n.385, s32[]{:T(128)S(6)} %select_n.386) | dynamic-update-slice | bytes 2097156 | tf_op jit(solution)/shard_map/while/body/dynamic_update_slice | solution.py:128
  647.8 2.5 fusion.709
  668.0 2.4 fusion.720
  690.0 11.3 %dynamic_update_slice.17 = f32[4,384,384]{2,1,0:T(8,128)} dynamic-update-slice(f32[4,384,384]{2,1,0:T(8,128)} %get-tuple-element.1071, f32[4,256,256]{2,1,0:T(8,128)S(1)} %maximum_add_fusion.10, s32[]{:T(128)} %constant.70.clone.1..sunk.1, s32[]{:T(128)S(6)} %select_n.385, s32[]{:T(128)S(6)} %select_n.386) | dynamic-update-slice | bytes 2097156 | tf_op jit(solution)/shard_map/while/body/dynamic_update_slice | solution.py:128
  706.2 2.5 fusion.709
  726.4 2.4 fusion.720
  748.5 11.5 %dynamic_update_slice.17 = f32[4,384,384]{2,1,0:T(8,128)} dynamic-update-slice(f32[4,384,384]{2,1,0:T(8,128)} %get-tuple-element.1071, f32[4,256,256]{2,1,0:T(8,128)S(1)} %maximum_add_fusion.10, s32[]{:T(128)} %constant.70.clone.1..sunk.1, s32[]{:T(128)S(6)} %select_n.385, s32[]{:T(128)S(6)} %select_n.386) | dynamic-update-slice | bytes 2097156 | tf_op jit(solution)/shard_map/while/body/dynamic_update_slice | solution.py:128
  765.8 119.2 %collective-permute-start.13 = (f32[4,64,384]{2,1,0:T(8,128)S(1)}, f32[4,64,384]{2,1,0:T(8,128)S(1)}, u32[]{:S(2)}, u32[]{:S(2)}) collective-permute-start(f32[4,64,384]{2,1,0:T(8,128)S(1)} %get-tuple-element.747), channel_id=1, source_target_pairs={{8,0},{16,8},{24,16},{0,24},{9,1},{17,9},{25,17},{1,25},{10,2},{18... | collective-permute-start | bytes 1179656 | tf_op jit(solution)/shard_map/ppermute | solution.py:25
  885.0 3.1 copy.30
  888.1 6.8 collective-permute-done.12
  895.5 2.5 pad_maximum_fusion.6
  898.1 3.4 collective-permute-start.15
  902.9 116.5 %all-reduce.13.cloned.1.call-done = f32[2,256,256]{2,1,0:T(8,128)} async-done(((f32[2,256,256]{2,1,0:T(8,128)}), f32[2,256,256]{2,1,0:T(8,128)}) %all-reduce.13.cloned.1.call-update) | async-done | bytes 524304 | tf_op jit(solution)/shard_map/psum | solution.py:142
  1021.3 2.9 pad_maximum_fusion.1
  (331 shorter events, 258.8 us)
Async XLA Ops:
  7.2 546.4 %all-reduce.11.cloned.1.call-start = ((), (), s32[]{:S(2)}) async-start(), calls=%async_computation | async-start | bytes 1048576 | tf_op jit(solution)/shard_map/psum | solution.py:142
  8.8 40.3 %copy-start.3 = (f32[2,2,256,256]{2,3,1,0:T(8,128)}, f32[2,2,256,256]{2,3,1,0:T(8,128)S(1)}, u32[]{:S(2)}) copy-start(f32[2,2,256,256]{2,3,1,0:T(8,128)S(1)} %copy.21) | copy-start | bytes 3145732
  10.0 16.9 %collective-permute-start = (f32[4,64,256]{1,2,0:T(8,128)}, f32[4,64,256]{1,2,0:T(8,128)S(1)}, u32[]{:S(2)}, u32[]{:S(2)}) collective-permute-start(f32[4,64,256]{1,2,0:T(8,128)} %get-tuple-element.756), channel_id=1, source_target_pairs={{0,8},{8,16},{16,24},{24,0},{1,9},{9,17},{17,25},{25,1},{2,10},{10... | collective-permute-start | bytes 786440 | tf_op jit(solution)/shard_map/ppermute | solution.py:22
  13.0 24.6 %collective-permute-start.1 = (f32[4,64,256]{1,2,0:T(8,128)}, f32[4,64,256]{1,2,0:T(8,128)S(1)}, u32[]{:S(2)}, u32[]{:S(2)}) collective-permute-start(f32[4,64,256]{1,2,0:T(8,128)} %get-tuple-element.757), channel_id=1, source_target_pairs={{8,0},{16,8},{24,16},{0,24},{9,1},{17,9},{25,17},{1,25},{10,2},{18... | collective-permute-start | bytes 786440 | tf_op jit(solution)/shard_map/ppermute | solution.py:25
  37.6 5.4 copy-start.12
  37.9 11.2 %collective-permute-start.2 = (f32[4,384,64]{1,2,0:T(8,128)S(1)}, f32[4,384,64]{1,2,0:T(8,128)S(1)}, u32[]{:S(2)}, u32[]{:S(2)}) collective-permute-start(f32[4,384,64]{1,2,0:T(8,128)S(1)} %get-tuple-element.752), channel_id=1, source_target_pairs={{0,1},{1,2},{2,3},{3,4},{4,5},{5,6},{6,7},{7,0},{8,9},{9,10},{10,1... | collective-permute-start | bytes 1179656 | tf_op jit(solution)/shard_map/ppermute | solution.py:22
  38.0 11.1 %collective-permute-start.3 = (f32[4,384,64]{1,2,0:T(8,128)S(1)}, f32[4,384,64]{1,2,0:T(8,128)S(1)}, u32[]{:S(2)}, u32[]{:S(2)}) collective-permute-start(f32[4,384,64]{1,2,0:T(8,128)S(1)} %get-tuple-element.753), channel_id=1, source_target_pairs={{1,0},{2,1},{3,2},{4,3},{5,4},{6,5},{7,6},{0,7},{9,8},{10,9},{11,1... | collective-permute-start | bytes 1179656 | tf_op jit(solution)/shard_map/ppermute | solution.py:25
  44.5 10.1 copy-start
  44.5 10.1 copy-start.13
  119.8 3.1 copy-start.9
  123.1 13.5 %copy-start.10 = (f32[2,256,256]{2,1,0:T(8,128)}, f32[2,256,256]{2,1,0:T(8,128)S(1)}, u32[]{:S(2)}) copy-start(f32[2,256,256]{2,1,0:T(8,128)S(1)} %maximum_add_fusion.9) | copy-start | bytes 1572868 | tf_op jit(solution)/shard_map/while
  177.8 3.1 copy-start.9
  181.1 13.3 %copy-start.10 = (f32[2,256,256]{2,1,0:T(8,128)}, f32[2,256,256]{2,1,0:T(8,128)S(1)}, u32[]{:S(2)}) copy-start(f32[2,256,256]{2,1,0:T(8,128)S(1)} %maximum_add_fusion.9) | copy-start | bytes 1572868 | tf_op jit(solution)/shard_map/while
  235.7 3.1 copy-start.9
  238.9 13.5 %copy-start.10 = (f32[2,256,256]{2,1,0:T(8,128)}, f32[2,256,256]{2,1,0:T(8,128)S(1)}, u32[]{:S(2)}) copy-start(f32[2,256,256]{2,1,0:T(8,128)S(1)} %maximum_add_fusion.9) | copy-start | bytes 1572868 | tf_op jit(solution)/shard_map/while
  259.3 124.5 %collective-permute-start.4 = (f32[4,64,384]{2,1,0:T(8,128)S(1)}, f32[4,64,384]{2,1,0:T(8,128)}, u32[]{:S(2)}, u32[]{:S(2)}) collective-permute-start(f32[4,64,384]{2,1,0:T(8,128)S(1)} %get-tuple-element.748), channel_id=1, source_target_pairs={{0,8},{8,16},{16,24},{24,0},{1,9},{9,17},{17,25},{25,1},{2,10},{10... | collective-permute-start | bytes 1179656 | tf_op jit(solution)/shard_map/ppermute | solution.py:22
  259.3 126.6 %collective-permute-start.5 = (f32[4,64,384]{2,1,0:T(8,128)S(1)}, f32[4,64,384]{2,1,0:T(8,128)S(1)}, u32[]{:S(2)}, u32[]{:S(2)}) collective-permute-start(f32[4,64,384]{2,1,0:T(8,128)S(1)} %get-tuple-element.749), channel_id=1, source_target_pairs={{8,0},{16,8},{24,16},{0,24},{9,1},{17,9},{25,17},{1,25},{10,2},{18... | collective-permute-start | bytes 1179656 | tf_op jit(solution)/shard_map/ppermute | solution.py:25
  388.7 13.5 %collective-permute-start.6 = (f32[4,512,64]{1,2,0:T(8,128)}, f32[4,512,64]{1,2,0:T(8,128)}, u32[]{:S(2)}, u32[]{:S(2)}) collective-permute-start(f32[4,512,64]{1,2,0:T(8,128)} %get-tuple-element.740), channel_id=1, source_target_pairs={{0,1},{1,2},{2,3},{3,4},{4,5},{5,6},{6,7},{7,0},{8,9},{9,10},{10,1... | collective-permute-start | bytes 1572872 | tf_op jit(solution)/shard_map/ppermute | solution.py:22
  393.0 11.9 %collective-permute-start.7 = (f32[4,512,64]{1,2,0:T(8,128)}, f32[4,512,64]{1,2,0:T(8,128)}, u32[]{:S(2)}, u32[]{:S(2)}) collective-permute-start(f32[4,512,64]{1,2,0:T(8,128)} %get-tuple-element.741), channel_id=1, source_target_pairs={{1,0},{2,1},{3,2},{4,3},{5,4},{6,5},{7,6},{0,7},{9,8},{10,9},{11,1... | collective-permute-start | bytes 1572872 | tf_op jit(solution)/shard_map/ppermute | solution.py:25
  394.3 13.6 %copy-start.2 = (f32[4,384,384]{1,2,0:T(8,128)S(1)}, f32[4,384,384]{1,2,0:T(8,128)}, u32[]{:S(2)}) copy-start(f32[4,384,384]{1,2,0:T(8,128)} %copy.25) | copy-start | bytes 7077892
  410.8 1.2 copy-start.4
  412.5 142.2 %copy-start.5 = (f32[4,256,256]{1,2,0:T(8,128)}, f32[4,256,256]{1,2,0:T(8,128)S(1)}, u32[]{:S(2)}) copy-start(f32[4,256,256]{1,2,0:T(8,128)S(1)} %fusion.249) | copy-start | bytes 3145732
  413.8 22.2 %collective-permute-start.8 = (f32[4,64,256]{1,2,0:T(8,128)}, f32[4,64,256]{1,2,0:T(8,128)S(1)}, u32[]{:S(2)}, u32[]{:S(2)}) collective-permute-start(f32[4,64,256]{1,2,0:T(8,128)} %get-tuple-element.754), channel_id=1, source_target_pairs={{0,8},{8,16},{16,24},{24,0},{1,9},{9,17},{17,25},{25,1},{2,10},{10... | collective-permute-start | bytes 786440 | tf_op jit(solution)/shard_map/ppermute | solution.py:22
  422.6 24.5 %collective-permute-start.9 = (f32[4,64,256]{1,2,0:T(8,128)}, f32[4,64,256]{1,2,0:T(8,128)}, u32[]{:S(2)}, u32[]{:S(2)}) collective-permute-start(f32[4,64,256]{1,2,0:T(8,128)} %get-tuple-element.755), channel_id=1, source_target_pairs={{8,0},{16,8},{24,16},{0,24},{9,1},{17,9},{25,17},{1,25},{10,2},{18... | collective-permute-start | bytes 786440 | tf_op jit(solution)/shard_map/ppermute | solution.py:25
  422.7 596.7 %all-reduce.13.cloned.1.call-start = ((), (), s32[]{:S(2)}) async-start(), calls=%async_computation.1 | async-start | bytes 1048576 | tf_op jit(solution)/shard_map/psum | solution.py:142
  436.0 17.0 %copy-start.11 = (f32[4,64,256]{1,2,0:T(8,128)}, f32[4,64,256]{1,2,0:T(8,128)S(1)}, u32[]{:S(2)}) copy-start(f32[4,64,256]{1,2,0:T(8,128)S(1)} %collective-permute-done.8) | copy-start | bytes 786436
  449.4 105.3 %collective-permute-start.10 = (f32[4,384,64]{1,2,0:T(8,128)}, f32[4,384,64]{1,2,0:T(8,128)S(1)}, u32[]{:S(2)}, u32[]{:S(2)}) collective-permute-start(f32[4,384,64]{1,2,0:T(8,128)} %get-tuple-element.750), channel_id=1, source_target_pairs={{0,1},{1,2},{2,3},{3,4},{4,5},{5,6},{6,7},{7,0},{8,9},{9,10},{10,1... | collective-permute-start | bytes 1179656 | tf_op jit(solution)/shard_map/ppermute | solution.py:22
  449.4 105.3 %collective-permute-start.11 = (f32[4,384,64]{1,2,0:T(8,128)}, f32[4,384,64]{1,2,0:T(8,128)}, u32[]{:S(2)}, u32[]{:S(2)}) collective-permute-start(f32[4,384,64]{1,2,0:T(8,128)} %get-tuple-element.751), channel_id=1, source_target_pairs={{1,0},{2,1},{3,2},{4,3},{5,4},{6,5},{7,6},{0,7},{9,8},{10,9},{11,1... | collective-permute-start | bytes 1179656 | tf_op jit(solution)/shard_map/ppermute | solution.py:25
  625.6 3.1 copy-start.7
  628.8 0.8 copy-start.8
  684.2 3.1 copy-start.7
  687.5 0.8 copy-start.8
  742.6 3.1 copy-start.7
  745.9 0.8 copy-start.8
  765.8 129.1 %collective-permute-start.12 = (f32[4,64,384]{2,1,0:T(8,128)S(1)}, f32[4,64,384]{2,1,0:T(8,128)S(1)}, u32[]{:S(2)}, u32[]{:S(2)}) collective-permute-start(f32[4,64,384]{2,1,0:T(8,128)S(1)} %get-tuple-element.746), channel_id=1, source_target_pairs={{0,8},{8,16},{16,24},{24,0},{1,9},{9,17},{17,25},{25,1},{2,10},{10... | collective-permute-start | bytes 1179656 | tf_op jit(solution)/shard_map/ppermute | solution.py:22
  765.8 129.3 %collective-permute-start.13 = (f32[4,64,384]{2,1,0:T(8,128)S(1)}, f32[4,64,384]{2,1,0:T(8,128)S(1)}, u32[]{:S(2)}, u32[]{:S(2)}) collective-permute-start(f32[4,64,384]{2,1,0:T(8,128)S(1)} %get-tuple-element.747), channel_id=1, source_target_pairs={{8,0},{16,8},{24,16},{0,24},{9,1},{17,9},{25,17},{1,25},{10,2},{18... | collective-permute-start | bytes 1179656 | tf_op jit(solution)/shard_map/ppermute | solution.py:25
  898.0 123.3 %collective-permute-start.14 = (f32[4,512,64]{1,2,0:T(8,128)}, f32[4,512,64]{1,2,0:T(8,128)S(1)}, u32[]{:S(2)}, u32[]{:S(2)}) collective-permute-start(f32[4,512,64]{1,2,0:T(8,128)} %get-tuple-element.738), channel_id=1, source_target_pairs={{0,1},{1,2},{2,3},{3,4},{4,5},{5,6},{6,7},{7,0},{8,9},{9,10},{10,1... | collective-permute-start | bytes 1572872 | tf_op jit(solution)/shard_map/ppermute | solution.py:22
  898.1 123.1 %collective-permute-start.15 = (f32[4,512,64]{1,2,0:T(8,128)}, f32[4,512,64]{1,2,0:T(8,128)S(1)}, u32[]{:S(2)}, u32[]{:S(2)}) collective-permute-start(f32[4,512,64]{1,2,0:T(8,128)} %get-tuple-element.739), channel_id=1, source_target_pairs={{1,0},{2,1},{3,2},{4,3},{5,4},{6,5},{7,6},{0,7},{9,8},{10,9},{11,1... | collective-permute-start | bytes 1572872 | tf_op jit(solution)/shard_map/ppermute | solution.py:25
  1021.2 3.0 copy-start.1
  1025.8 1.2 copy-start.6
Sparse Core Ops, SparseCore 0:
  422.8 130.7 all-reduce.10
  888.2 131.0 all-reduce.12
where the time goes:
time: 1050 us; the launch traced here: 1040 us
  waiting for transfers between devices  289 us (28%)
  starting transfers between devices  264 us (25%)
  matrix products  211 us (20%)
  local copies, waits for them, and re-layouts  128 us (12%)
  loops' own time  85.2 us (8%)
  other arithmetic  42.3 us (4%)
  between operations  15.9 us (2%)
    ppermute x8, starting transfers between devices, extended_2(): lax.ppermute(lax.slice_in_dim(block, 0, width, axis=dim), axis, backward)  248 us
    psum x2, waiting for transfers between devices, body(): summed = lax.psum(probe_grad, ('ty', 'tx'))  217 us
    dot_general x196, matrix products, matmul(): jnp.dot(left, right, precision=lax.Precision.HIGHEST, preferred_element_t...  211 us
    another operation x2, loops' own time, body(): grads, probe_grad = lax.fori_loop(zero, count, visit, start)  85.2 us
    dynamic_update_slice x6, local copies, waits for them, and re-layouts, visit(): lax.dynamic_update_slice(local, current + object_part, (zero, top, left))  68.5 us
    ppermute x8, waiting for transfers between devices, extended_2(): lax.ppermute(lax.slice_in_dim(block, block.shape[dim] - width, None, axis...  46.6 us
    ppermute x8, waiting for transfers between devices, extended_2(): lax.ppermute(lax.slice_in_dim(block, 0, width, axis=dim), axis, backward)  25.5 us
  transfers between devices with their start and end apart: 18, of which 12 were waited for; matrix products, arithmetic and copies ran while one was open for 2% of the time, Pallas kernels for 0%

commit v1 on v0

--- a/solution.py
+++ b/solution.py
@@ -139,7 +139,7 @@
         core = core - object_rate / peak * total
         if step + 1 < ITERS:
             extended = extended_2(core, (("ty", 1), ("tx", 2)), MARGIN)
-        summed = lax.psum(probe_grad, ("ty", "tx"))
+        summed = lax.psum(lax.psum(probe_grad, "tx"), "ty")
         probe_now = probe_now - probe_rate / devices * summed
     return (core.reshape(2, 2, CORE, CORE), probe_now)
 

time: 1050 us -> 975 us (0.929)
  waiting for transfers between devices: 289 us -> 223 us
    psum x2 -> x4, waiting for transfers between devices: 217 us -> 167 us  [body(): summed = lax.psum(lax.psum(probe_grad, 'tx'), 'ty')]
    ppermute x8, waiting for transfers between devices: 46.6 us -> 33.5 us  [extended_2(): lax.ppermute(lax.slice_in_dim(block, block.shape[dim] - width, None, axis...]
  transfers between devices with their start and end apart: 18 -> 20, of which waited for: 12 -> 11; matrix products, arithmetic and copies ran while one was open for 2% -> 3% of each run, Pallas kernels for 0% -> 0%
where the time goes in v1:
time: 975 us; the launch traced here: 963 us
  starting transfers between devices  258 us (26%)
  waiting for transfers between devices  223 us (23%)
  matrix products  211 us (22%)
  local copies, waits for them, and re-layouts  128 us (13%)
  loops' own time  86.4 us (9%)
  other arithmetic  41.5 us (4%)
  between operations  15.6 us (2%)
    ppermute x8, starting transfers between devices, extended_2(): lax.ppermute(lax.slice_in_dim(block, 0, width, axis=dim), axis, backward)  249 us
    dot_general x196, matrix products, matmul(): jnp.dot(left, right, precision=lax.Precision.HIGHEST, preferred_element_t...  211 us
    psum x4, waiting for transfers between devices, body(): summed = lax.psum(lax.psum(probe_grad, 'tx'), 'ty')  167 us
    another operation x2, loops' own time, body(): grads, probe_grad = lax.fori_loop(zero, count, visit, start)  86.4 us
    dynamic_update_slice x6, local copies, waits for them, and re-layouts, visit(): lax.dynamic_update_slice(local, current + object_part, (zero, top, left))  68.5 us
    ppermute x8, waiting for transfers between devices, extended_2(): lax.ppermute(lax.slice_in_dim(block, block.shape[dim] - width, None, axis...  33.5 us
    ppermute x8, waiting for transfers between devices, extended_2(): lax.ppermute(lax.slice_in_dim(block, 0, width, axis=dim), axis, backward)  21.9 us
  transfers between devices with their start and end apart: 20, of which 11 were waited for; matrix products, arithmetic and copies ran while one was open for 3% of the time, Pallas kernels for 0%

profile of v1, /device:TPU:0, one launch (start us, length us, event | category | flops | bytes accessed | tf_op | source)
XLA Modules:
  0.0 962.9 jit_solution(12940458433252814597)
XLA Ops:
  10.1 3.0 collective-permute-start
  17.2 9.8 %collective-permute-done = f32[4,64,256]{1,2,0:T(8,128)S(1)} collective-permute-done((f32[4,64,256]{1,2,0:T(8,128)}, f32[4,64,256]{1,2,0:T(8,128)S(1)}, u32[]{:S(2)}, u32[]{:S(2)}) %collective-permute-start) | collective-permute-done | bytes 262176 | tf_op jit(solution)/shard_map/ppermute | solution.py:22
  27.0 10.6 %collective-permute-done.1 = f32[4,64,256]{1,2,0:T(8,128)S(1)} collective-permute-done((f32[4,64,256]{1,2,0:T(8,128)}, f32[4,64,256]{1,2,0:T(8,128)S(1)}, u32[]{:S(2)}, u32[]{:S(2)}) %collective-permute-start.1) | collective-permute-done | bytes 262176 | tf_op jit(solution)/shard_map/ppermute | solution.py:25
  38.0 3.5 collective-permute-start.3
  44.5 4.6 collective-permute-done.2
  49.1 3.1 pad_maximum_fusion.2
  54.7 204.0 %while.32 = (s32[]{:T(128)}, f32[4,384,384]{2,1,0:T(8,128)}, f32[2,256,256]{2,1,0:T(8,128)}, s32[]{:T(128)}, s32[1,1,5,2]{2,3,1,0:T(2,128)S(1)}, /*index=5*/f32[...) while((s32[]{:T(128)}, f32[4,384,384]{2,1,0:T(8,128)}, ...), condition=%wide.region_2.3_spmd.clone.clone, body=%wide.region_1.2_spmd.clone.clone.sunk | while | flops 6464077824 | bytes 48234916 | solution.py:135
  83.6 2.5 fusion.635
  103.9 2.4 fusion.646
  123.3 2.0 maximum_add_fusion.8
  125.3 11.5 %dynamic_update_slice.16 = f32[4,384,384]{2,1,0:T(8,128)} dynamic-update-slice(f32[4,384,384]{2,1,0:T(8,128)} %get-tuple-element.1014, f32[4,256,256]{2,1,0:T(8,128)S(1)} %maximum_add_fusion.8, s32[]{:T(128)} %constant.70.clone.1..sunk, s32[]{:T(128)S(6)} %select_n.366, s32[]{:T(128)S(6)} %select_n.367) | dynamic-update-slice | bytes 2097156 | tf_op jit(solution)/shard_map/while/body/dynamic_update_slice | solution.py:128
  141.8 2.5 fusion.635
  162.1 2.4 fusion.646
  183.5 11.2 %dynamic_update_slice.16 = f32[4,384,384]{2,1,0:T(8,128)} dynamic-update-slice(f32[4,384,384]{2,1,0:T(8,128)} %get-tuple-element.1014, f32[4,256,256]{2,1,0:T(8,128)S(1)} %maximum_add_fusion.8, s32[]{:T(128)} %constant.70.clone.1..sunk, s32[]{:T(128)S(6)} %select_n.366, s32[]{:T(128)S(6)} %select_n.367) | dynamic-update-slice | bytes 2097156 | tf_op jit(solution)/shard_map/while/body/dynamic_update_slice | solution.py:128
  199.8 2.5 fusion.635
  220.0 2.4 fusion.646
  239.5 2.0 maximum_add_fusion.8
  241.5 11.5 %dynamic_update_slice.16 = f32[4,384,384]{2,1,0:T(8,128)} dynamic-update-slice(f32[4,384,384]{2,1,0:T(8,128)} %get-tuple-element.1014, f32[4,256,256]{2,1,0:T(8,128)S(1)} %maximum_add_fusion.8, s32[]{:T(128)} %constant.70.clone.1..sunk, s32[]{:T(128)S(6)} %select_n.366, s32[]{:T(128)S(6)} %select_n.367) | dynamic-update-slice | bytes 2097156 | tf_op jit(solution)/shard_map/while/body/dynamic_update_slice | solution.py:128
  259.9 117.3 %collective-permute-start.5 = (f32[4,64,384]{2,1,0:T(8,128)S(1)}, f32[4,64,384]{2,1,0:T(8,128)S(1)}, u32[]{:S(2)}, u32[]{:S(2)}) collective-permute-start(f32[4,64,384]{2,1,0:T(8,128)S(1)} %get-tuple-element.749), channel_id=1, source_target_pairs={{8,0},{16,8},{24,16},{0,24},{9,1},{17,9},{25,17},{1,25},{10,2},{18... | collective-permute-start | bytes 1179656 | tf_op jit(solution)/shard_map/ppermute | solution.py:25
  377.2 3.1 copy.25
  380.3 4.3 collective-permute-done.4
  387.0 2.5 pad_maximum_fusion.9
  389.5 4.3 collective-permute-start.6
  395.2 63.5 %all-reduce.13.cloned.1.call-done = f32[2,256,256]{2,1,0:T(8,128)} async-done(((f32[2,256,256]{2,1,0:T(8,128)}), f32[2,256,256]{2,1,0:T(8,128)}) %all-reduce.13.cloned.1.call-update) | async-done | bytes 524304 | tf_op jit(solution)/shard_map/psum | solution.py:142
  458.8 3.2 pad_maximum_fusion
  462.0 2.8 fusion.242
  469.8 14.8 %collective-permute-done.8 = f32[4,64,256]{1,2,0:T(8,128)S(1)} collective-permute-done((f32[4,64,256]{1,2,0:T(8,128)S(1)}, f32[4,64,256]{1,2,0:T(8,128)S(1)}, u32[]{:S(2)}, u32[]{:S(2)}) %collective-permute-start.8) | collective-permute-done | bytes 262176 | tf_op jit(solution)/shard_map/ppermute | solution.py:22
  484.6 10.3 %collective-permute-done.9 = f32[4,64,256]{1,2,0:T(8,128)S(1)} collective-permute-done((f32[4,64,256]{1,2,0:T(8,128)S(1)}, f32[4,64,256]{1,2,0:T(8,128)S(1)}, u32[]{:S(2)}, u32[]{:S(2)}) %collective-permute-start.9) | collective-permute-done | bytes 262176 | tf_op jit(solution)/shard_map/ppermute | solution.py:25
  496.9 3.5 collective-permute-start.11
  500.4 10.1 %all-reduce.15.cloned.1.call-done = f32[2,256,256]{2,1,0:T(8,128)} async-done(((f32[2,256,256]{2,1,0:T(8,128)}), f32[2,256,256]{2,1,0:T(8,128)}) %all-reduce.15.cloned.1.call-update) | async-done | bytes 524304 | tf_op jit(solution)/shard_map/psum | solution.py:142
  511.6 3.4 pad_maximum_fusion.3
  517.4 204.6 %while.33 = (s32[]{:T(128)}, f32[4,384,384]{2,1,0:T(8,128)}, f32[2,256,256]{2,1,0:T(8,128)}, s32[]{:T(128)}, s32[1,1,5,2]{2,3,1,0:T(2,128)S(1)}, /*index=5*/f32[...) while((s32[]{:T(128)}, f32[4,384,384]{2,1,0:T(8,128)}, ...), condition=%wide.region_7.8_spmd.clone.clone, body=%wide.region_6.7_spmd.clone.clone.sunk | while | flops 6464077824 | bytes 48234916 | solution.py:135
  546.3 2.5 fusion.709
  566.5 2.4 fusion.720
  588.5 11.5 %dynamic_update_slice.17 = f32[4,384,384]{2,1,0:T(8,128)} dynamic-update-slice(f32[4,384,384]{2,1,0:T(8,128)} %get-tuple-element.1071, f32[4,256,256]{2,1,0:T(8,128)S(1)} %maximum_add_fusion.10, s32[]{:T(128)} %constant.70.clone.1..sunk.1, s32[]{:T(128)S(6)} %select_n.385, s32[]{:T(128)S(6)} %select_n.386) | dynamic-update-slice | bytes 2097156 | tf_op jit(solution)/shard_map/while/body/dynamic_update_slice | solution.py:128
  605.1 2.5 fusion.709
  625.3 2.4 fusion.720
  647.3 11.2 %dynamic_update_slice.17 = f32[4,384,384]{2,1,0:T(8,128)} dynamic-update-slice(f32[4,384,384]{2,1,0:T(8,128)} %get-tuple-element.1071, f32[4,256,256]{2,1,0:T(8,128)S(1)} %maximum_add_fusion.10, s32[]{:T(128)} %constant.70.clone.1..sunk.1, s32[]{:T(128)S(6)} %select_n.385, s32[]{:T(128)S(6)} %select_n.386) | dynamic-update-slice | bytes 2097156 | tf_op jit(solution)/shard_map/while/body/dynamic_update_slice | solution.py:128
  663.6 2.5 fusion.709
  683.9 2.4 fusion.720
  705.9 11.5 %dynamic_update_slice.17 = f32[4,384,384]{2,1,0:T(8,128)} dynamic-update-slice(f32[4,384,384]{2,1,0:T(8,128)} %get-tuple-element.1071, f32[4,256,256]{2,1,0:T(8,128)S(1)} %maximum_add_fusion.10, s32[]{:T(128)} %constant.70.clone.1..sunk.1, s32[]{:T(128)S(6)} %select_n.385, s32[]{:T(128)S(6)} %select_n.386) | dynamic-update-slice | bytes 2097156 | tf_op jit(solution)/shard_map/while/body/dynamic_update_slice | solution.py:128
  723.3 118.5 %collective-permute-start.13 = (f32[4,64,384]{2,1,0:T(8,128)S(1)}, f32[4,64,384]{2,1,0:T(8,128)S(1)}, u32[]{:S(2)}, u32[]{:S(2)}) collective-permute-start(f32[4,64,384]{2,1,0:T(8,128)S(1)} %get-tuple-element.747), channel_id=1, source_target_pairs={{8,0},{16,8},{24,16},{0,24},{9,1},{17,9},{25,17},{1,25},{10,2},{18... | collective-permute-start | bytes 1179656 | tf_op jit(solution)/shard_map/ppermute | solution.py:25
  841.9 57.4 %all-reduce.17.cloned.1.call-done = f32[2,256,256]{2,1,0:T(8,128)} async-done(((f32[2,256,256]{2,1,0:T(8,128)}), f32[2,256,256]{2,1,0:T(8,128)}) %all-reduce.17.cloned.1.call-update) | async-done | bytes 524304 | tf_op jit(solution)/shard_map/psum | solution.py:142
  899.3 3.1 copy.30
  902.9 2.5 pad_maximum_fusion.6
  905.4 3.5 collective-permute-start.15
  910.3 36.3 %all-reduce.19.cloned.1.call-done = f32[2,256,256]{2,1,0:T(8,128)} async-done(((f32[2,256,256]{2,1,0:T(8,128)}), f32[2,256,256]{2,1,0:T(8,128)}) %all-reduce.19.cloned.1.call-update) | async-done | bytes 524304 | tf_op jit(solution)/shard_map/psum | solution.py:142
  948.5 2.9 pad_maximum_fusion.1
  (339 shorter events, 256.7 us)
Async XLA Ops:
  7.2 451.6 %all-reduce.13.cloned.1.call-start = ((), (), s32[]{:S(2)}) async-start(), calls=%async_computation | async-start | bytes 1048576 | tf_op jit(solution)/shard_map/psum | solution.py:142
  8.8 40.4 %copy-start.3 = (f32[2,2,256,256]{2,3,1,0:T(8,128)}, f32[2,2,256,256]{2,3,1,0:T(8,128)S(1)}, u32[]{:S(2)}) copy-start(f32[2,2,256,256]{2,3,1,0:T(8,128)S(1)} %copy.21) | copy-start | bytes 3145732
  10.1 16.9 %collective-permute-start = (f32[4,64,256]{1,2,0:T(8,128)}, f32[4,64,256]{1,2,0:T(8,128)S(1)}, u32[]{:S(2)}, u32[]{:S(2)}) collective-permute-start(f32[4,64,256]{1,2,0:T(8,128)} %get-tuple-element.756), channel_id=1, source_target_pairs={{0,8},{8,16},{16,24},{24,0},{1,9},{9,17},{17,25},{25,1},{2,10},{10... | collective-permute-start | bytes 786440 | tf_op jit(solution)/shard_map/ppermute | solution.py:22
  13.1 24.6 %collective-permute-start.1 = (f32[4,64,256]{1,2,0:T(8,128)}, f32[4,64,256]{1,2,0:T(8,128)S(1)}, u32[]{:S(2)}, u32[]{:S(2)}) collective-permute-start(f32[4,64,256]{1,2,0:T(8,128)} %get-tuple-element.757), channel_id=1, source_target_pairs={{8,0},{16,8},{24,16},{0,24},{9,1},{17,9},{25,17},{1,25},{10,2},{18... | collective-permute-start | bytes 786440 | tf_op jit(solution)/shard_map/ppermute | solution.py:25
  37.6 5.4 copy-start.11
  38.0 11.2 %collective-permute-start.2 = (f32[4,384,64]{1,2,0:T(8,128)S(1)}, f32[4,384,64]{1,2,0:T(8,128)S(1)}, u32[]{:S(2)}, u32[]{:S(2)}) collective-permute-start(f32[4,384,64]{1,2,0:T(8,128)S(1)} %get-tuple-element.752), channel_id=1, source_target_pairs={{0,1},{1,2},{2,3},{3,4},{4,5},{5,6},{6,7},{7,0},{8,9},{9,10},{10,1... | collective-permute-start | bytes 1179656 | tf_op jit(solution)/shard_map/ppermute | solution.py:22
  38.0 11.1 %collective-permute-start.3 = (f32[4,384,64]{1,2,0:T(8,128)S(1)}, f32[4,384,64]{1,2,0:T(8,128)S(1)}, u32[]{:S(2)}, u32[]{:S(2)}) collective-permute-start(f32[4,384,64]{1,2,0:T(8,128)S(1)} %get-tuple-element.753), channel_id=1, source_target_pairs={{1,0},{2,1},{3,2},{4,3},{5,4},{6,5},{7,6},{0,7},{9,8},{10,9},{11,1... | collective-permute-start | bytes 1179656 | tf_op jit(solution)/shard_map/ppermute | solution.py:25
  44.5 10.1 %copy-start = (f32[2,256,256]{2,1,0:T(8,128)S(1)}, f32[2,256,256]{2,1,0:T(8,128)}, u32[]{:S(2)}) copy-start(f32[2,256,256]{2,1,0:T(8,128)} %param.10) | copy-start | bytes 1572868
  44.5 10.1 %copy-start.14 = (s32[1,1,5,2]{2,3,1,0:T(2,128)S(1)}, s32[1,1,5,2]{2,3,1,0:T(2,128)}, u32[]{:S(2)}) copy-start(s32[1,1,5,2]{2,3,1,0:T(2,128)} %param.12) | copy-start | bytes 124
  120.0 3.1 copy-start.9
  123.3 13.5 %copy-start.10 = (f32[2,256,256]{2,1,0:T(8,128)}, f32[2,256,256]{2,1,0:T(8,128)S(1)}, u32[]{:S(2)}) copy-start(f32[2,256,256]{2,1,0:T(8,128)S(1)} %maximum_add_fusion.9) | copy-start | bytes 1572868 | tf_op jit(solution)/shard_map/while
  178.2 3.1 copy-start.9
  181.5 13.2 %copy-start.10 = (f32[2,256,256]{2,1,0:T(8,128)}, f32[2,256,256]{2,1,0:T(8,128)S(1)}, u32[]{:S(2)}) copy-start(f32[2,256,256]{2,1,0:T(8,128)S(1)} %maximum_add_fusion.9) | copy-start | bytes 1572868 | tf_op jit(solution)/shard_map/while
  236.2 3.1 copy-start.9
  239.5 13.5 %copy-start.10 = (f32[2,256,256]{2,1,0:T(8,128)}, f32[2,256,256]{2,1,0:T(8,128)S(1)}, u32[]{:S(2)}) copy-start(f32[2,256,256]{2,1,0:T(8,128)S(1)} %maximum_add_fusion.9) | copy-start | bytes 1572868 | tf_op jit(solution)/shard_map/while
  259.9 124.7 %collective-permute-start.4 = (f32[4,64,384]{2,1,0:T(8,128)S(1)}, f32[4,64,384]{2,1,0:T(8,128)}, u32[]{:S(2)}, u32[]{:S(2)}) collective-permute-start(f32[4,64,384]{2,1,0:T(8,128)S(1)} %get-tuple-element.748), channel_id=1, source_target_pairs={{0,8},{8,16},{16,24},{24,0},{1,9},{9,17},{17,25},{25,1},{2,10},{10... | collective-permute-start | bytes 1179656 | tf_op jit(solution)/shard_map/ppermute | solution.py:22
  259.9 126.8 %collective-permute-start.5 = (f32[4,64,384]{2,1,0:T(8,128)S(1)}, f32[4,64,384]{2,1,0:T(8,128)S(1)}, u32[]{:S(2)}, u32[]{:S(2)}) collective-permute-start(f32[4,64,384]{2,1,0:T(8,128)S(1)} %get-tuple-element.749), channel_id=1, source_target_pairs={{8,0},{16,8},{24,16},{0,24},{9,1},{17,9},{25,17},{1,25},{10,2},{18... | collective-permute-start | bytes 1179656 | tf_op jit(solution)/shard_map/ppermute | solution.py:25
  389.5 69.3 %collective-permute-start.6 = (f32[4,512,64]{1,2,0:T(8,128)}, f32[4,512,64]{1,2,0:T(8,128)}, u32[]{:S(2)}, u32[]{:S(2)}) collective-permute-start(f32[4,512,64]{1,2,0:T(8,128)} %get-tuple-element.740), channel_id=1, source_target_pairs={{0,1},{1,2},{2,3},{3,4},{4,5},{5,6},{6,7},{7,0},{8,9},{9,10},{10,1... | collective-permute-start | bytes 1572872 | tf_op jit(solution)/shard_map/ppermute | solution.py:22
  393.8 65.0 %collective-permute-start.7 = (f32[4,512,64]{1,2,0:T(8,128)}, f32[4,512,64]{1,2,0:T(8,128)}, u32[]{:S(2)}, u32[]{:S(2)}) collective-permute-start(f32[4,512,64]{1,2,0:T(8,128)} %get-tuple-element.741), channel_id=1, source_target_pairs={{1,0},{2,1},{3,2},{4,3},{5,4},{6,5},{7,6},{0,7},{9,8},{10,9},{11,1... | collective-permute-start | bytes 1572872 | tf_op jit(solution)/shard_map/ppermute | solution.py:25
  393.9 116.6 %all-reduce.15.cloned.1.call-start = ((), (), s32[]{:S(2)}) async-start(), calls=%async_computation.1 | async-start | bytes 1048576 | tf_op jit(solution)/shard_map/psum | solution.py:142
  458.8 440.5 %all-reduce.17.cloned.1.call-start = ((), (), s32[]{:S(2)}) async-start(), calls=%async_computation.2 | async-start | bytes 1048576 | tf_op jit(solution)/shard_map/psum | solution.py:142
  458.8 3.2 copy-start.1
  464.9 1.2 copy-start.4
  466.6 45.0 %copy-start.5 = (f32[4,256,256]{1,2,0:T(8,128)}, f32[4,256,256]{1,2,0:T(8,128)S(1)}, u32[]{:S(2)}) copy-start(f32[4,256,256]{1,2,0:T(8,128)S(1)} %fusion.249) | copy-start | bytes 3145732
  466.8 17.8 %collective-permute-start.8 = (f32[4,64,256]{1,2,0:T(8,128)S(1)}, f32[4,64,256]{1,2,0:T(8,128)S(1)}, u32[]{:S(2)}, u32[]{:S(2)}) collective-permute-start(f32[4,64,256]{1,2,0:T(8,128)S(1)} %get-tuple-element.754), channel_id=1, source_target_pairs={{0,8},{8,16},{16,24},{24,0},{1,9},{9,17},{17,25},{25,1},{2,10},{10... | collective-permute-start | bytes 786440 | tf_op jit(solution)/shard_map/ppermute | solution.py:22
  468.3 26.5 %collective-permute-start.9 = (f32[4,64,256]{1,2,0:T(8,128)S(1)}, f32[4,64,256]{1,2,0:T(8,128)S(1)}, u32[]{:S(2)}, u32[]{:S(2)}) collective-permute-start(f32[4,64,256]{1,2,0:T(8,128)S(1)} %get-tuple-element.755), channel_id=1, source_target_pairs={{8,0},{16,8},{24,16},{0,24},{9,1},{17,9},{25,17},{1,25},{10,2},{18... | collective-permute-start | bytes 786440 | tf_op jit(solution)/shard_map/ppermute | solution.py:25
  484.6 15.9 %copy-start.12 = (f32[4,64,256]{1,2,0:T(8,128)}, f32[4,64,256]{1,2,0:T(8,128)S(1)}, u32[]{:S(2)}) copy-start(f32[4,64,256]{1,2,0:T(8,128)S(1)} %collective-permute-done.8) | copy-start | bytes 786436
  494.8 0.8 copy-start.13
  496.9 14.7 %collective-permute-start.10 = (f32[4,384,64]{1,2,0:T(8,128)}, f32[4,384,64]{1,2,0:T(8,128)S(1)}, u32[]{:S(2)}, u32[]{:S(2)}) collective-permute-start(f32[4,384,64]{1,2,0:T(8,128)} %get-tuple-element.750), channel_id=1, source_target_pairs={{0,1},{1,2},{2,3},{3,4},{4,5},{5,6},{6,7},{7,0},{8,9},{9,10},{10,1... | collective-permute-start | bytes 1179656 | tf_op jit(solution)/shard_map/ppermute | solution.py:22
  496.9 14.7 %collective-permute-start.11 = (f32[4,384,64]{1,2,0:T(8,128)}, f32[4,384,64]{1,2,0:T(8,128)}, u32[]{:S(2)}, u32[]{:S(2)}) collective-permute-start(f32[4,384,64]{1,2,0:T(8,128)} %get-tuple-element.751), channel_id=1, source_target_pairs={{1,0},{2,1},{3,2},{4,3},{5,4},{6,5},{7,6},{0,7},{9,8},{10,9},{11,1... | collective-permute-start | bytes 1179656 | tf_op jit(solution)/shard_map/ppermute | solution.py:25
  582.7 3.1 copy-start.7
  585.9 0.8 copy-start.8
  641.5 3.1 copy-start.7
  644.7 0.8 copy-start.8
  700.0 3.1 copy-start.7
  703.3 0.8 copy-start.8
  723.3 179.1 %collective-permute-start.12 = (f32[4,64,384]{2,1,0:T(8,128)S(1)}, f32[4,64,384]{2,1,0:T(8,128)S(1)}, u32[]{:S(2)}, u32[]{:S(2)}) collective-permute-start(f32[4,64,384]{2,1,0:T(8,128)S(1)} %get-tuple-element.746), channel_id=1, source_target_pairs={{0,8},{8,16},{16,24},{24,0},{1,9},{9,17},{17,25},{25,1},{2,10},{10... | collective-permute-start | bytes 1179656 | tf_op jit(solution)/shard_map/ppermute | solution.py:22
  723.3 179.3 %collective-permute-start.13 = (f32[4,64,384]{2,1,0:T(8,128)S(1)}, f32[4,64,384]{2,1,0:T(8,128)S(1)}, u32[]{:S(2)}, u32[]{:S(2)}) collective-permute-start(f32[4,64,384]{2,1,0:T(8,128)S(1)} %get-tuple-element.747), channel_id=1, source_target_pairs={{8,0},{16,8},{24,16},{0,24},{9,1},{17,9},{25,17},{1,25},{10,2},{18... | collective-permute-start | bytes 1179656 | tf_op jit(solution)/shard_map/ppermute | solution.py:25
  841.8 104.8 %all-reduce.19.cloned.1.call-start = ((), (), s32[]{:S(2)}) async-start(), calls=%async_computation.3 | async-start | bytes 1048576 | tf_op jit(solution)/shard_map/psum | solution.py:142
  905.4 43.1 %collective-permute-start.14 = (f32[4,512,64]{1,2,0:T(8,128)}, f32[4,512,64]{1,2,0:T(8,128)S(1)}, u32[]{:S(2)}, u32[]{:S(2)}) collective-permute-start(f32[4,512,64]{1,2,0:T(8,128)} %get-tuple-element.738), channel_id=1, source_target_pairs={{0,1},{1,2},{2,3},{3,4},{4,5},{5,6},{6,7},{7,0},{8,9},{9,10},{10,1... | collective-permute-start | bytes 1572872 | tf_op jit(solution)/shard_map/ppermute | solution.py:22
  905.4 43.1 %collective-permute-start.15 = (f32[4,512,64]{1,2,0:T(8,128)}, f32[4,512,64]{1,2,0:T(8,128)S(1)}, u32[]{:S(2)}, u32[]{:S(2)}) collective-permute-start(f32[4,512,64]{1,2,0:T(8,128)} %get-tuple-element.739), channel_id=1, source_target_pairs={{1,0},{2,1},{3,2},{4,3},{5,4},{6,5},{7,6},{0,7},{9,8},{10,9},{11,1... | collective-permute-start | bytes 1572872 | tf_op jit(solution)/shard_map/ppermute | solution.py:25
  948.5 3.0 copy-start.2
  953.1 1.2 copy-start.6
Sparse Core Ops, SparseCore 0:
  394.1 64.6 all-reduce.12
  461.7 48.7 all-reduce.14
  841.9 57.2 all-reduce.16
  902.1 44.4 all-reduce.18
